TPU v7x, 32 devices: a whole 2x2x4 slice. The times are simulated.
32 devices in a mesh: grp: 8 (over y, x, core), tp: 4 (over z).
Axes of the slice: x: 2, y: 2, z: 4, core: 2. Of those that a mesh axis runs over, the one named last changes fastest.
Arguments:
- tokens: bfloat16 [4096, 6144], P('grp'), may hold values from -40 to 40
- norm_gain: bfloat16 [6144], replicated, may hold values from 0.099609375 to 1.8984375
- up_weight: bfloat16 [6144, 12288], P('grp', 'tp'), may hold values from -0.078125 to 0.078125
- up_bias: float32 [12288], P('tp'), may hold values from -3 to 3
- down_weight: bfloat16 [12288, 6144], P('tp', 'grp'), may hold values from -0.0546875 to 0.0546875
- down_bias: float32 [6144], P('tp'), may hold values from -2 to 2
Outputs:
- encoded: bfloat16 [4096, 6144], P('grp', 'tp')
All inputs are finite; a program needn't handle non-finite values.
Results may differ from a plain program's by a relative error of at most 0.0085.
Values may be sent and summed in bfloat16 or wider, within the bound.
A program may use at most 128 MiB of HBM per device.

v0:
```python
import functools

import jax
import jax.numpy as jnp
from jax import lax
from jax.experimental import pallas as pl
from jax.experimental.pallas import tpu as pltpu
from jax.sharding import PartitionSpec as P

MESH = pl.DeviceIdType.MESH
HID_CHUNK = 512
COL_CHUNK = 128
EARLY_V = 2


def chunk_of(extent, wanted):
    step = min(wanted, extent)
    while extent % step:
        step -= 128
    return step


def dot(a, b):
    return jnp.dot(a, b, preferred_element_type=jnp.float32)


def build(groups, planes):
    bits = groups.bit_length() - 1
    k_bit, n_bit = bits - 1, 1
    up_bits = [b for b in range(1, bits) if b != k_bit] + [0]
    down_bits = [b for b in range(bits - 1, 0, -1) if b != n_bit] + [0]
    per_plane = groups // planes
    pieces = groups // 2
    slots = planes // 2

    def masks_of(order):
        masks = [()]
        for bit in order:
            masks = masks + [m + (bit,) for m in masks]
        return masks

    up_masks, down_masks = masks_of(up_bits), masks_of(down_bits)

    def stages_from(piece, order):
        return [s for s in range(len(order)) if (1 << s) > piece]

    def kernel(
        tok, gain, w, ubias, v, dbias, out, vh,
        tk, sh, xo, xp, wb, ps, pr, acc, hid, hx, zu, zd, fr, ob, *rest,
    ):
        rest = list(rest)
        vb = rest.pop(0) if len(rest) == 26 else wb
        (gv, ub, db, tk_sem, misc_sem, wl_sem, vl_sem,
         up_send, up_recv, dn_send, dn_recv, x_send, x_recv,
         zxu_send, zxu_recv, zxd_send, zxd_recv,
         p_send, p_recv, h_send, h_recv, z_send, zu_recv, zd_recv, f_sem) = rest
        f_send, f_recv = f_sem.at[0], f_sem.at[1]

        me = lax.axis_index("grp")
        z = lax.axis_index("tp")
        rows, width = tok.shape
        depth, hidden = w.shape
        out_block = v.shape[1]
        own_width = out.shape[1]
        half = width // 2
        chunks, _, hj = wb.shape
        cols = vb.shape[2] // pieces
        col_chunks = vb.shape[0]
        slot_width = per_plane * cols
        shard = rows // planes

        def bit_of(b):
            return (me // (1 << b)) % 2

        def flipped(index_bits):
            index = me
            for b in index_bits:
                index = index + (1 - 2 * bit_of(b)) * (1 << b)
            return index

        def near(b):
            return {"grp": flipped((b,))}

        k_half, n_half = bit_of(k_bit), bit_of(n_bit)

        def up_place(mask):
            return pl.multiple_of((flipped(mask) % pieces) * depth, depth)

        def down_place(mask):
            block = flipped(mask)
            return pl.multiple_of(((block // 4) * 2 + block % 2) * cols, cols)

        def up_copy(j, piece, stage):
            place = pl.ds(up_place(up_masks[piece]), depth)
            landing = wb.at[j, place, :]
            source = w.at[:, pl.ds(pl.multiple_of(j * hj, hj), hj)] if piece == 0 else landing
            slot = piece + (1 << stage) - 1
            return pltpu.make_async_remote_copy(
                src_ref=source, dst_ref=landing,
                send_sem=up_send.at[j, slot], recv_sem=up_recv.at[j, slot],
                device_id=near(up_bits[stage]), device_id_type=MESH)

        def up_arrival(j, piece):
            place = pl.ds(up_place(up_masks[piece]), depth)
            landing = wb.at[j, place, :]
            stage = piece.bit_length() - 1
            return pltpu.make_async_remote_copy(
                src_ref=landing, dst_ref=landing,
                send_sem=up_send.at[j, piece - 1], recv_sem=up_recv.at[j, piece - 1],
                device_id=near(up_bits[stage]), device_id_type=MESH)

        def w_local(j):
            return pltpu.make_async_copy(
                w.at[:, pl.ds(pl.multiple_of(j * hj, hj), hj)],
                wb.at[j, pl.ds(up_place(()), depth), :], wl_sem.at[j])

        def down_copy(q, piece, stage):
            place = pl.ds(down_place(down_masks[piece]), cols)
            landing = vh.at[q, :, place]
            source = v.at[:, pl.ds(pl.multiple_of(q * cols, cols), cols)] if piece == 0 else landing
            slot = piece + (1 << stage) - 1
            return pltpu.make_async_remote_copy(
                src_ref=source, dst_ref=landing,
                send_sem=dn_send.at[q, slot], recv_sem=dn_recv.at[q, slot],
                device_id=near(down_bits[stage]), device_id_type=MESH)

        def down_arrival(q, piece):
            landing = vh.at[q, :, pl.ds(down_place(down_masks[piece]), cols)]
            stage = piece.bit_length() - 1
            return pltpu.make_async_remote_copy(
                src_ref=landing, dst_ref=landing,
                send_sem=dn_send.at[q, piece - 1], recv_sem=dn_recv.at[q, piece - 1],
                device_id=near(down_bits[stage]), device_id_type=MESH)

        def v_local(q, piece):
            place = pl.ds(down_place(down_masks[piece]), cols)
            source = v.at[:, pl.ds(pl.multiple_of(q * cols, cols), cols)] if piece == 0 else vh.at[q, :, place]
            return pltpu.make_async_copy(source, vb.at[q, :, place], vl_sem.at[q, piece])

        barrier = pltpu.get_barrier_semaphore()
        for b in range(bits):
            pl.semaphore_signal(barrier, inc=1, device_id=near(b), device_id_type=MESH)

        @pl.when(z > 0)
        def _():
            pl.semaphore_signal(barrier, inc=1, device_id={"tp": z - 1}, device_id_type=MESH)

        @pl.when(z < planes - 1)
        def _():
            pl.semaphore_signal(barrier, inc=1, device_id={"tp": z + 1}, device_id_type=MESH)

        shard_rows = pl.ds(pl.multiple_of(z * shard, shard), shard)

        def token_copy(index, slot):
            source = shard_rows if index < 0 else pl.ds(index * shard, shard)
            return pltpu.make_async_copy(tok.at[source, :], tk.at[slot], tk_sem.at[slot])

        token_copy(-1, 0).start()
        token_copy(0, 1).start()
        small = [
            pltpu.make_async_copy(gain, gv, misc_sem.at[0]),
            pltpu.make_async_copy(ubias, ub, misc_sem.at[1]),
            pltpu.make_async_copy(dbias, db, misc_sem.at[2]),
            pltpu.make_async_copy(
                tok.at[:, pl.ds(pl.multiple_of(z * own_width, own_width), own_width)], ob, misc_sem.at[3]),
        ]
        for copy in small:
            copy.start()

        neighbours = bits + jnp.where(z > 0, 1, 0) + jnp.where(z < planes - 1, 1, 0)
        pl.semaphore_wait(barrier, neighbours)

        def start_up(j, carry):
            for stage in range(len(up_bits)):
                up_copy(j, 0, stage).start()
            w_local(j).start()
            return carry

        lax.fori_loop(0, chunks, start_up, 0)
        small[0].wait()

        tile = 16

        def normalise(slot, column, dst, base):
            def body(i, carry):
                at = pl.multiple_of(i * tile, tile)
                values = tk[slot, pl.ds(at, tile), :].astype(jnp.float32)
                centre = jnp.mean(values, axis=1, keepdims=True)
                shifted = values - centre
                scale = lax.rsqrt(jnp.mean(shifted * shifted, axis=1, keepdims=True) + 1e-06)
                part = tk[slot, pl.ds(at, tile), pl.ds(column, half)].astype(jnp.float32)
                normed = (part - centre) * scale * gv[:, pl.ds(column, half)].astype(jnp.float32)
                dst[pl.ds(pl.multiple_of(base + at, tile), tile), :] = normed.astype(jnp.bfloat16)
                return carry

            lax.fori_loop(0, shard // tile, body, 0)

        own_column = pl.multiple_of(k_half * half, half)
        other_column = pl.multiple_of((1 - k_half) * half, half)

        token_copy(-1, 0).wait()
        normalise(0, other_column, sh, 0)
        shard_send = pltpu.make_async_remote_copy(
            src_ref=sh, dst_ref=xp.at[shard_rows, :],
            send_sem=x_send, recv_sem=x_recv, device_id=near(k_bit), device_id_type=MESH)
        shard_send.start()

        def start_down(q):
            down_copy(q, 0, 0).start()

        early = min(EARLY_V, col_chunks)
        for q in range(early):
            start_down(q)

        def start_down_core(q, carry):
            for stage in range(1, len(down_bits)):
                down_copy(q, 0, stage).start()
            return carry

        for c in range(planes):
            slot = (c + 1) % 2
            if c + 1 < planes:
                token_copy(c + 1, 1 - slot).start()
            token_copy(c, slot).wait()
            normalise(slot, own_column, xo, c * shard)

        shard_send.wait_recv()

        def pass_on(distance, rising):
            source = z - distance if rising else z + distance
            place = pl.ds(pl.multiple_of(source * shard, shard), shard)
            return pltpu.make_async_remote_copy(
                src_ref=xp.at[place, :], dst_ref=xp.at[place, :],
                send_sem=(zxu_send if rising else zxd_send).at[distance],
                recv_sem=(zxu_recv if rising else zxd_recv).at[distance],
                device_id={"tp": z + 1 if rising else z - 1}, device_id_type=MESH)

        def arrival(distance, rising):
            source = z - distance if rising else z + distance
            place = pl.ds(pl.multiple_of(source * shard, shard), shard)
            return pltpu.make_async_remote_copy(
                src_ref=xp.at[place, :], dst_ref=xp.at[place, :],
                send_sem=(zxu_send if rising else zxd_send).at[distance - 1],
                recv_sem=(zxu_recv if rising else zxd_recv).at[distance - 1],
                device_id={"tp": z - 1 if rising else z + 1}, device_id_type=MESH)

        for distance in range(planes):
            if distance:
                @pl.when(z >= distance)
                def _():
                    arrival(distance, True).wait_recv()

                @pl.when(z + distance <= planes - 1)
                def _():
                    arrival(distance, False).wait_recv()

            if distance < planes - 1:
                @pl.when((z >= distance) & (z < planes - 1))
                def _():
                    pass_on(distance, True).start()

                @pl.when((z + distance <= planes - 1) & (z > 0))
                def _():
                    pass_on(distance, False).start()

        shard_send.wait_send()
        small[1].wait()

        row_tile = min(256, rows)
        row_tiles = rows // row_tile

        def partial_copy(j):
            return pltpu.make_async_remote_copy(
                src_ref=ps.at[j, :, pl.ds(0, hj)], dst_ref=pr.at[j], send_sem=p_send.at[j], recv_sem=p_recv.at[j],
                device_id=near(k_bit), device_id_type=MESH)

        def hidden_copy(j):
            place = pl.ds(pl.multiple_of(j * hj, hj), hj)
            return pltpu.make_async_remote_copy(
                src_ref=hid.at[:, place], dst_ref=hx.at[:, place], send_sem=h_send.at[j], recv_sem=h_recv.at[j],
                device_id=near(n_bit), device_id_type=MESH)

        def finish(j):
            partial_copy(j).wait_recv()
            place = pl.ds(pl.multiple_of(j * hj, hj), hj)

            def body(i, carry):
                at = pl.ds(pl.multiple_of(i * 64, 64), 64)
                pre = acc[j % 2, at, pl.ds(0, hj)] + pr[j, at, :].astype(jnp.float32) + ub[:, place]
                hid[at, place] = jax.nn.gelu(pre, approximate=True).astype(jnp.bfloat16)
                return carry

            lax.fori_loop(0, rows // 64, body, 0)
            hidden_copy(j).start()

        def up_step(j, carry):
            for piece in range(1, pieces):
                stages = stages_from(piece, up_bits)
                if stages:
                    up_arrival(j, piece).wait_recv()
                    for stage in stages:
                        up_copy(j, piece, stage).start()

            @pl.when(j > 0)
            def _():
                finish(j - 1)

            for piece in range(1, pieces):
                if not stages_from(piece, up_bits):
                    up_arrival(j, piece).wait_recv()
            w_local(j).wait()

            def sent(i, carry):
                at = pl.ds(pl.multiple_of(i * row_tile, row_tile), row_tile)
                ps[j, at, pl.ds(0, hj)] = dot(xp[at, :], wb[j]).astype(jnp.bfloat16)
                return carry

            lax.fori_loop(0, row_tiles, sent, 0)
            partial_copy(j).start()

            def kept(i, carry):
                at = pl.ds(pl.multiple_of(i * row_tile, row_tile), row_tile)
                acc[j % 2, at, pl.ds(0, hj)] = dot(xo[at, :], wb[j])
                return carry

            lax.fori_loop(0, row_tiles, kept, 0)
            return carry

        lax.fori_loop(0, chunks, up_step, 0)
        for q in range(early, col_chunks):
            start_down(q)
        lax.fori_loop(0, col_chunks, start_down_core, 0)
        finish(chunks - 1)

        def settle_up(j, carry):
            for piece in range(pieces):
                for stage in stages_from(piece, up_bits):
                    up_copy(j, piece, stage).wait_send()
            partial_copy(j).wait_send()
            return carry

        lax.fori_loop(0, chunks, settle_up, 0)
        small[2].wait()
        small[3].wait()

        def target(u):
            return 2 * u + n_half

        def z_up(item, q, u):
            return pltpu.make_async_remote_copy(
                src_ref=ps.at[q, :, pl.ds(u * slot_width, slot_width)], dst_ref=zu.at[item, u],
                send_sem=z_send.at[item, u], recv_sem=zu_recv.at[item, u],
                device_id={"tp": z + 1}, device_id_type=MESH)

        def z_down(item, q, u):
            return pltpu.make_async_remote_copy(
                src_ref=ps.at[q, :, pl.ds(u * slot_width, slot_width)], dst_ref=zd.at[item, u],
                send_sem=z_send.at[item, u], recv_sem=zd_recv.at[item, u],
                device_id={"tp": z - 1}, device_id_type=MESH)

        def final_copy(q, u):
            return pltpu.make_async_remote_copy(
                src_ref=ps.at[q, :, pl.ds(u * slot_width, slot_width)], dst_ref=fr.at[q],
                send_sem=f_send.at[q], recv_sem=f_recv.at[q],
                device_id=near(n_bit), device_id_type=MESH)

        def deliver(q, value_of):
            for c in range(per_plane):
                place = pl.ds(pl.multiple_of(c * out_block + q * cols, cols), cols)

                def body(i, carry):
                    at = pl.ds(pl.multiple_of(i * 64, 64), 64)
                    total = ob[at, place].astype(jnp.float32) + value_of(at, c) + db[:, place]
                    ob[at, place] = total.astype(jnp.bfloat16)
                    return carry

                lax.fori_loop(0, rows // 64, body, 0)

        def chain(item, q, mine):
            buf = item % 2
            for u in range(slots):
                to = target(u)
                lanes = pl.ds(u * slot_width, slot_width)

                @pl.when((z > 0) & (z <= to))
                def _():
                    z_up(item, q, u).wait_recv()
                    acc[buf, :, lanes] = acc[buf, :, lanes] + zu[item, u].astype(jnp.float32)

                @pl.when((z < planes - 1) & (z >= to))
                def _():
                    z_down(item, q, u).wait_recv()
                    acc[buf, :, lanes] = acc[buf, :, lanes] + zd[item, u].astype(jnp.float32)

                @pl.when(z != to)
                def _():
                    if not mine:
                        z_up(item - col_chunks, q, u).wait_send()
                    ps[q, :, lanes] = acc[buf, :, lanes].astype(jnp.bfloat16)

                @pl.when(z < to)
                def _():
                    z_up(item, q, u).start()

                @pl.when(z > to)
                def _():
                    z_down(item, q, u).start()

                @pl.when(z == to)
                def _():
                    if mine:
                        deliver(q, lambda at, c: acc[buf, at, pl.ds(u * slot_width + c * cols, cols)])
                    else:
                        ps[q, :, lanes] = acc[buf, :, lanes].astype(jnp.bfloat16)
                        final_copy(q, u).start()

        def down_dot(src, item, q):
            def body(i, carry):
                at = pl.ds(pl.multiple_of(i * row_tile, row_tile), row_tile)
                acc[item % 2, at, pl.ds(0, cols * pieces)] = dot(src[at, :], vb[q])
                return carry

            lax.fori_loop(0, row_tiles, body, 0)

        def own_step(q, carry):
            for piece in range(1, pieces):
                stages = stages_from(piece, down_bits)
                if stages:
                    down_arrival(q, piece).wait_recv()
                    for stage in stages:
                        down_copy(q, piece, stage).start()
                    v_local(q, piece).start()
            v_local(q, 0).start()

            @pl.when(q > 0)
            def _():
                chain(q - 1, q - 1, True)

            for piece in range(1, pieces):
                if not stages_from(piece, down_bits):
                    down_arrival(q, piece).wait_recv()
                    v_local(q, piece).start()
            for piece in range(pieces):
                v_local(q, piece).wait()
            down_dot(hid, q, q)
            return carry

        lax.fori_loop(0, col_chunks, own_step, 0)
        chain(col_chunks - 1, col_chunks - 1, True)

        def hidden_arrives(j, carry):
            hidden_copy(j).wait_recv()
            return carry

        lax.fori_loop(0, chunks, hidden_arrives, 0)

        def other_step(q, carry):
            down_dot(hx, col_chunks + q, q)

            @pl.when(q > 0)
            def _():
                chain(col_chunks + q - 1, q - 1, False)
            return carry

        lax.fori_loop(0, col_chunks, other_step, 0)
        chain(2 * col_chunks - 1, col_chunks - 1, False)

        @pl.when(z % 2 != n_half)
        def _():
            def body(q, carry):
                final_copy(q, 0).wait_recv()
                deliver(q, lambda at, c: fr[q, at, pl.ds(c * cols, cols)].astype(jnp.float32))
                return carry

            lax.fori_loop(0, col_chunks, body, 0)

        write = pltpu.make_async_copy(ob, out, misc_sem.at[0])
        write.start()

        def settle_down(q, carry):
            for piece in range(pieces):
                for stage in stages_from(piece, down_bits):
                    down_copy(q, piece, stage).wait_send()
            for u in range(slots):
                @pl.when(z != target(u))
                def _():
                    z_up(col_chunks + q, q, u).wait_send()

                @pl.when(z == target(u))
                def _():
                    final_copy(q, u).wait_send()
            return carry

        lax.fori_loop(0, col_chunks, settle_down, 0)

        def settle_hidden(j, carry):
            hidden_copy(j).wait_send()
            return carry

        lax.fori_loop(0, chunks, settle_hidden, 0)
        for distance in range(planes - 1):
            @pl.when((z >= distance) & (z < planes - 1))
            def _():
                pass_on(distance, True).wait_send()

            @pl.when((z + distance <= planes - 1) & (z > 0))
            def _():
                pass_on(distance, False).wait_send()
        write.wait()

    def per_device(tokens, norm_gain, up_weight, up_bias, down_weight, down_bias):
        rows, width = tokens.shape
        depth, hidden = up_weight.shape
        out_block = down_weight.shape[1]
        own_width = down_bias.shape[0]
        hj = chunk_of(hidden, HID_CHUNK)
        cols = chunk_of(out_block, COL_CHUNK)
        chunks, col_chunks = hidden // hj, out_block // cols
        half, shard = width // 2, rows // planes
        slab = cols * pieces
        bf, f32 = jnp.bfloat16, jnp.float32
        dma = pltpu.SemaphoreType.DMA
        shared = (chunks, half, hj) == (col_chunks, hidden, slab)
        scratch = [
            pltpu.VMEM((2, shard, width), bf),
            pltpu.VMEM((shard, half), bf),
            pltpu.VMEM((rows, half), bf),
            pltpu.VMEM((rows, half), bf),
            pltpu.VMEM((chunks, half, hj), bf),
            pltpu.VMEM((max(chunks, col_chunks), rows, max(hj, slab)), bf),
            pltpu.VMEM((chunks, rows, hj), bf),
            pltpu.VMEM((2, rows, max(hj, slab)), f32),
            pltpu.VMEM((rows, hidden), bf),
            pltpu.VMEM((rows, hidden), bf),
            pltpu.VMEM((2 * col_chunks, slots, rows, per_plane * cols), bf),
            pltpu.VMEM((2 * col_chunks, slots, rows, per_plane * cols), bf),
            pltpu.VMEM((col_chunks, rows, per_plane * cols), bf),
            pltpu.VMEM((rows, own_width), bf),
        ]
        if not shared:
            scratch.append(pltpu.VMEM((col_chunks, hidden, slab), bf))
        scratch += [
            pltpu.VMEM((1, width), bf),
            pltpu.VMEM((1, hidden), f32),
            pltpu.VMEM((1, own_width), f32),
            dma((2,)), dma((4,)), dma((chunks,)), dma((col_chunks, pieces)),
            dma((chunks, pieces - 1)), dma((chunks, pieces - 1)),
            dma((col_chunks, pieces - 1)), dma((col_chunks, pieces - 1)),
            dma, dma,
            dma((planes,)), dma((planes,)), dma((planes,)), dma((planes,)),
            dma((chunks,)), dma((chunks,)), dma((chunks,)), dma((chunks,)),
            dma((2 * col_chunks, slots)), dma((2 * col_chunks, slots)), dma((2 * col_chunks, slots)),
            dma((2, col_chunks)),
        ]
        hbm = pl.BlockSpec(memory_space=pltpu.HBM)
        result, _ = pl.pallas_call(
            kernel,
            out_shape=(
                jax.ShapeDtypeStruct((rows, own_width), bf),
                jax.ShapeDtypeStruct((col_chunks, hidden, slab), bf),
            ),
            in_specs=[hbm] * 6,
            out_specs=(hbm, hbm),
            scratch_shapes=scratch,
            compiler_params=pltpu.CompilerParams(
                collective_id=0, has_side_effects=True, vmem_limit_bytes=67043328),
        )(tokens, norm_gain[None, :], up_weight, up_bias[None, :], down_weight, down_bias[None, :])
        return result

    return per_device


def solution(mesh):
    in_specs = (P("grp", None), P(), P("grp", "tp"), P("tp"), P("tp", "grp"), P("tp"))
    return jax.shard_map(
        build(mesh.shape["grp"], mesh.shape["tp"]),
        mesh=mesh, in_specs=in_specs, out_specs=P("grp", "tp"), check_vma=False,
    )
```

profile of v0, /device:TPU:18, one launch (start us, length us, event | category | flops | bytes accessed | tf_op | source)
XLA Modules:
  0.0 514.3 jit_solution(15085070082421367891)
XLA Ops:
  0.0 1.3 broadcast_in_dim.11.dbias
  1.3 1.3 broadcast_in_dim.9.gain
  2.6 509.0 %shard_map.64 = (bf16[512,1536]{1,0:T(8,128)(2,1)}, bf16[6,3072,512]{2,1,0:T(8,128)(2,1)}) custom-call(bf16[512,6144]{1,0:T(8,128)(2,1)} %tok.1, bf16[1,6144]{1,0:T(2,128)(2,1)} %broadcast_in_dim.9.gain, bf16[768,3072]{1,0:T(8,128)(2,1)} %w.1, f32[1,3072]{1,0:T(1,128)} %bitcast.1, bf16[3072,768]{1,0:T(8,128)(2,1)} %v.1, f32[1,1536]{1,0:T(1,128)} %broadcast_in_dim.11.dbias), custom_call_target="tpu_custom_call" | custom-call | tf_op jit(solution)/shard_map/pallas_call | solution.py:556
  511.6 2.7 copy.8
where the time goes:
time: 515 us; the launch traced here: 514 us
  Pallas kernels  509 us (99%)
  local copies, waits for them, and re-layouts  5.28 us (1%)
    pallas_call x1, Pallas kernels, per_device(): pl.pallas_call(kernel, out_shape=(jax.ShapeDtypeStruct((rows, own_width),...  509 us

commit v1 on v0

--- a/solution.py
+++ b/solution.py
@@ -10,7 +10,8 @@
 MESH = pl.DeviceIdType.MESH
 HID_CHUNK = 512
 COL_CHUNK = 128
-EARLY_V = 2
+ROW_SPLIT = 2
+EARLY_V = (-1, 1)
 
 
 def chunk_of(extent, wanted):
@@ -46,15 +47,15 @@
 
     def kernel(
         tok, gain, w, ubias, v, dbias, out, vh,
-        tk, sh, xo, xp, wb, ps, pr, acc, hid, hx, zu, zd, fr, ob, *rest,
+        tk, sh, xo, xp, wb, ps, pr, acc, hid, hx, zu, zd, fr, cr, ob, *rest,
     ):
         rest = list(rest)
-        vb = rest.pop(0) if len(rest) == 26 else wb
+        vb = rest.pop(0) if len(rest) == 27 else wb
         (gv, ub, db, tk_sem, misc_sem, wl_sem, vl_sem,
          up_send, up_recv, dn_send, dn_recv, x_send, x_recv,
          zxu_send, zxu_recv, zxd_send, zxd_recv,
-         p_send, p_recv, h_send, h_recv, z_send, zu_recv, zd_recv, f_sem) = rest
-        f_send, f_recv = f_sem.at[0], f_sem.at[1]
+         p_send, p_recv, h_send, h_recv, z_send, zu_recv, zd_recv, f_sem, c_sem) = rest
+        f_send, f_recv, c_send, c_recv = f_sem.at[0], f_sem.at[1], c_sem.at[0], c_sem.at[1]
 
         me = lax.axis_index("grp")
         z = lax.axis_index("tp")
@@ -208,9 +209,10 @@
         def start_down(q):
             down_copy(q, 0, 0).start()
 
-        early = min(EARLY_V, col_chunks)
-        for q in range(early):
-            start_down(q)
+        early = [q for q in range(len(EARLY_V)) if q < col_chunks]
+        for q in early:
+            if EARLY_V[q] < 0:
+                start_down(q)
 
         def start_down_core(q, carry):
             for stage in range(1, len(down_bits)):
@@ -224,8 +226,6 @@
             token_copy(c, slot).wait()
             normalise(slot, own_column, xo, c * shard)
 
-        shard_send.wait_recv()
-
         def pass_on(distance, rising):
             source = z - distance if rising else z + distance
             place = pl.ds(pl.multiple_of(source * shard, shard), shard)
@@ -244,34 +244,34 @@
                 recv_sem=(zxu_recv if rising else zxd_recv).at[distance - 1],
                 device_id={"tp": z - 1 if rising else z + 1}, device_id_type=MESH)
 
-        for distance in range(planes):
-            if distance:
-                @pl.when(z >= distance)
-                def _():
-                    arrival(distance, True).wait_recv()
-
-                @pl.when(z + distance <= planes - 1)
-                def _():
-                    arrival(distance, False).wait_recv()
-
-            if distance < planes - 1:
-                @pl.when((z >= distance) & (z < planes - 1))
-                def _():
-                    pass_on(distance, True).start()
-
-                @pl.when((z + distance <= planes - 1) & (z > 0))
-                def _():
-                    pass_on(distance, False).start()
-
-        shard_send.wait_send()
+        def pass_tokens(distance):
+            @pl.when(distance == 0)
+            def _():
+                shard_send.wait_recv()
+
+            @pl.when((distance > 0) & (z >= distance))
+            def _():
+                arrival(distance, True).wait_recv()
+
+            @pl.when((distance > 0) & (z + distance <= planes - 1))
+            def _():
+                arrival(distance, False).wait_recv()
+
+            @pl.when((z >= distance) & (z < planes - 1) & (distance < planes - 1))
+            def _():
+                pass_on(distance, True).start()
+
+            @pl.when((z + distance <= planes - 1) & (z > 0) & (distance < planes - 1))
+            def _():
+                pass_on(distance, False).start()
+
         small[1].wait()
 
-        row_tile = min(256, rows)
-        row_tiles = rows // row_tile
-
-        def partial_copy(j):
-            return pltpu.make_async_remote_copy(
-                src_ref=ps.at[j, :, pl.ds(0, hj)], dst_ref=pr.at[j], send_sem=p_send.at[j], recv_sem=p_recv.at[j],
+        def partial_copy(j, block):
+            place = pl.ds(pl.multiple_of(block * shard, shard), shard)
+            return pltpu.make_async_remote_copy(
+                src_ref=ps.at[j, place, pl.ds(0, hj)], dst_ref=pr.at[j, place, :],
+                send_sem=p_send.at[j, block], recv_sem=p_recv.at[j, block],
                 device_id=near(k_bit), device_id_type=MESH)
 
         def hidden_copy(j):
@@ -280,199 +280,243 @@
                 src_ref=hid.at[:, place], dst_ref=hx.at[:, place], send_sem=h_send.at[j], recv_sem=h_recv.at[j],
                 device_id=near(n_bit), device_id_type=MESH)
 
+        row_tile = min(256, rows)
+
         def finish(j):
-            partial_copy(j).wait_recv()
             place = pl.ds(pl.multiple_of(j * hj, hj), hj)
+
+            def kept(i, carry):
+                at = pl.ds(pl.multiple_of(i * row_tile, row_tile), row_tile)
+                acc[at, :] = dot(xo[at, :], wb[j])
+                return carry
+
+            lax.fori_loop(0, rows // row_tile, kept, 0)
+            for block in range(planes):
+                partial_copy(j, block).wait_recv()
 
             def body(i, carry):
                 at = pl.ds(pl.multiple_of(i * 64, 64), 64)
-                pre = acc[j % 2, at, pl.ds(0, hj)] + pr[j, at, :].astype(jnp.float32) + ub[:, place]
+                pre = acc[at, :] + pr[j, at, :].astype(jnp.float32) + ub[:, place]
                 hid[at, place] = jax.nn.gelu(pre, approximate=True).astype(jnp.bfloat16)
                 return carry
 
             lax.fori_loop(0, rows // 64, body, 0)
             hidden_copy(j).start()
 
-        def up_step(j, carry):
-            for piece in range(1, pieces):
-                stages = stages_from(piece, up_bits)
-                if stages:
-                    up_arrival(j, piece).wait_recv()
-                    for stage in stages:
-                        up_copy(j, piece, stage).start()
-
-            @pl.when(j > 0)
-            def _():
-                finish(j - 1)
-
-            for piece in range(1, pieces):
-                if not stages_from(piece, up_bits):
-                    up_arrival(j, piece).wait_recv()
-            w_local(j).wait()
-
-            def sent(i, carry):
-                at = pl.ds(pl.multiple_of(i * row_tile, row_tile), row_tile)
-                ps[j, at, pl.ds(0, hj)] = dot(xp[at, :], wb[j]).astype(jnp.bfloat16)
+        rounds = max(planes, chunks)
+
+        def up_step(m, carry):
+            @pl.when(m < chunks)
+            def _():
+                for piece in range(1, pieces):
+                    stages = stages_from(piece, up_bits)
+                    if stages:
+                        up_arrival(m, piece).wait_recv()
+                        for stage in stages:
+                            up_copy(m, piece, stage).start()
+
+            @pl.when(m < planes)
+            def _():
+                pass_tokens(m)
+
+            @pl.when(m < chunks)
+            def _():
+                for piece in range(1, pieces):
+                    if not stages_from(piece, up_bits):
+                        up_arrival(m, piece).wait_recv()
+                w_local(m).wait()
+
+            def sent(t, carry):
+                distance = jnp.where(t // 2 < m, t // 2, m)
+                j = jnp.where(t // 2 <= m, m, t // 2 - m - 1)
+                block = jnp.where(t % 2 == 0, z - distance, z + distance)
+
+                @pl.when((block >= 0) & (block < planes) & (j < chunks) & ((t % 2 == 0) | (distance > 0)))
+                def _():
+                    at = pl.ds(pl.multiple_of(block * shard, shard), shard)
+                    ps[j, at, pl.ds(0, hj)] = dot(xp[at, :], wb[j]).astype(jnp.bfloat16)
+                    partial_copy(j, block).start()
                 return carry
 
-            lax.fori_loop(0, row_tiles, sent, 0)
-            partial_copy(j).start()
-
-            def kept(i, carry):
-                at = pl.ds(pl.multiple_of(i * row_tile, row_tile), row_tile)
-                acc[j % 2, at, pl.ds(0, hj)] = dot(xo[at, :], wb[j])
-                return carry
-
-            lax.fori_loop(0, row_tiles, kept, 0)
-            return carry
-
-        lax.fori_loop(0, chunks, up_step, 0)
-        for q in range(early, col_chunks):
+            lax.fori_loop(0, 2 * (2 * m + 1), sent, 0)
+            for q in early:
+                @pl.when(m == EARLY_V[q])
+                def _():
+                    start_down(q)
+
+            for j in range(2):
+                @pl.when((m >= planes) & (2 * (m - planes) + j < chunks))
+                def _():
+                    finish(2 * (m - planes) + j)
+            return carry
+
+        lax.fori_loop(0, rounds, up_step, 0)
+        for q in range(len(early), col_chunks):
             start_down(q)
         lax.fori_loop(0, col_chunks, start_down_core, 0)
-        finish(chunks - 1)
+
+        def finish_rest(j, carry):
+            finish(j)
+            return carry
+
+        lax.fori_loop(min(2 * (rounds - planes), chunks), chunks, finish_rest, 0)
+        shard_send.wait_send()
 
         def settle_up(j, carry):
             for piece in range(pieces):
                 for stage in stages_from(piece, up_bits):
                     up_copy(j, piece, stage).wait_send()
-            partial_copy(j).wait_send()
+            for block in range(planes):
+                partial_copy(j, block).wait_send()
             return carry
 
         lax.fori_loop(0, chunks, settle_up, 0)
         small[2].wait()
         small[3].wait()
 
-        def target(u):
-            return 2 * u + n_half
-
-        def z_up(item, q, u):
-            return pltpu.make_async_remote_copy(
-                src_ref=ps.at[q, :, pl.ds(u * slot_width, slot_width)], dst_ref=zu.at[item, u],
-                send_sem=z_send.at[item, u], recv_sem=zu_recv.at[item, u],
-                device_id={"tp": z + 1}, device_id_type=MESH)
-
-        def z_down(item, q, u):
-            return pltpu.make_async_remote_copy(
-                src_ref=ps.at[q, :, pl.ds(u * slot_width, slot_width)], dst_ref=zd.at[item, u],
-                send_sem=z_send.at[item, u], recv_sem=zd_recv.at[item, u],
-                device_id={"tp": z - 1}, device_id_type=MESH)
-
-        def final_copy(q, u):
-            return pltpu.make_async_remote_copy(
-                src_ref=ps.at[q, :, pl.ds(u * slot_width, slot_width)], dst_ref=fr.at[q],
-                send_sem=f_send.at[q], recv_sem=f_recv.at[q],
+        part = rows // ROW_SPLIT
+        items = col_chunks * ROW_SPLIT
+        crossed = n_half * (slots - 1)
+        entering = 2 * ((1 - n_half) * (slots - 1)) + 1 - n_half
+
+        def rows_of(i):
+            return pl.ds(pl.multiple_of((i % ROW_SPLIT) * part, part), part)
+
+        def lanes_of(u):
+            return pl.ds(pl.multiple_of(u * slot_width, slot_width), slot_width)
+
+        def sums(i, u, other):
+            return ps.at[i // ROW_SPLIT + col_chunks * other, rows_of(i), lanes_of(u)]
+
+        def z_copy(i, lane, src, up):
+            return pltpu.make_async_remote_copy(
+                src_ref=src, dst_ref=(zu if up else zd).at[lane, i],
+                send_sem=z_send.at[lane, i], recv_sem=(zu_recv if up else zd_recv).at[lane, i],
+                device_id={"tp": z + 1 if up else z - 1}, device_id_type=MESH)
+
+        def final_copy(i, u):
+            return pltpu.make_async_remote_copy(
+                src_ref=sums(i, u, 1), dst_ref=fr.at[i], send_sem=f_send.at[i], recv_sem=f_recv.at[i],
                 device_id=near(n_bit), device_id_type=MESH)
 
-        def deliver(q, value_of):
+        def cross_copy(i):
+            return pltpu.make_async_remote_copy(
+                src_ref=sums(i, crossed, 1), dst_ref=cr.at[i], send_sem=c_send.at[i], recv_sem=c_recv.at[i],
+                device_id=near(n_bit), device_id_type=MESH)
+
+        def deliver(i, value):
+            at = rows_of(i)
             for c in range(per_plane):
-                place = pl.ds(pl.multiple_of(c * out_block + q * cols, cols), cols)
-
-                def body(i, carry):
-                    at = pl.ds(pl.multiple_of(i * 64, 64), 64)
-                    total = ob[at, place].astype(jnp.float32) + value_of(at, c) + db[:, place]
-                    ob[at, place] = total.astype(jnp.bfloat16)
-                    return carry
-
-                lax.fori_loop(0, rows // 64, body, 0)
-
-        def chain(item, q, mine):
-            buf = item % 2
-            for u in range(slots):
-                to = target(u)
-                lanes = pl.ds(u * slot_width, slot_width)
+                place = pl.ds(pl.multiple_of(c * out_block + (i // ROW_SPLIT) * cols, cols), cols)
+                total = ob[at, place].astype(jnp.float32) + value[:, pl.ds(c * cols, cols)].astype(jnp.float32)
+                ob[at, place] = (total + db[:, place]).astype(jnp.bfloat16)
+
+        def depth_of(to):
+            above = planes - 1 - z
+            return jnp.where(z < to, z, jnp.where(z > to, above, jnp.where(z > above, z, above)))
+
+        def lane_source(i, lane):
+            if lane < slots:
+                return sums(i, lane, 0), 2 * lane + n_half
+            if lane < 2 * slots - 1:
+                u = lane - slots + 1 - n_half
+                return sums(i, u, 1), 2 * u + n_half
+            return cr.at[i], entering
+
+        def chain(s, lane):
+            _, to = lane_source(0, lane)
+            late = 1 if lane < slots else items + 1 if lane < 2 * slots - 1 else items + 2
+            i = s - late - depth_of(to)
+
+            @pl.when((i >= 0) & (i < items))
+            def _():
+                src, _ = lane_source(i, lane)
+                if lane == 2 * slots - 1:
+                    cross_copy(i).wait_recv()
 
                 @pl.when((z > 0) & (z <= to))
                 def _():
-                    z_up(item, q, u).wait_recv()
-                    acc[buf, :, lanes] = acc[buf, :, lanes] + zu[item, u].astype(jnp.float32)
+                    z_copy(i, lane, src, True).wait_recv()
+                    src[...] = (src[...].astype(jnp.float32) + zu[lane, i].astype(jnp.float32)).astype(jnp.bfloat16)
 
                 @pl.when((z < planes - 1) & (z >= to))
                 def _():
-                    z_down(item, q, u).wait_recv()
-                    acc[buf, :, lanes] = acc[buf, :, lanes] + zd[item, u].astype(jnp.float32)
-
-                @pl.when(z != to)
-                def _():
-                    if not mine:
-                        z_up(item - col_chunks, q, u).wait_send()
-                    ps[q, :, lanes] = acc[buf, :, lanes].astype(jnp.bfloat16)
+                    z_copy(i, lane, src, False).wait_recv()
+                    src[...] = (src[...].astype(jnp.float32) + zd[lane, i].astype(jnp.float32)).astype(jnp.bfloat16)
 
                 @pl.when(z < to)
                 def _():
-                    z_up(item, q, u).start()
+                    z_copy(i, lane, src, True).start()
 
                 @pl.when(z > to)
                 def _():
-                    z_down(item, q, u).start()
+                    z_copy(i, lane, src, False).start()
 
                 @pl.when(z == to)
                 def _():
-                    if mine:
-                        deliver(q, lambda at, c: acc[buf, at, pl.ds(u * slot_width + c * cols, cols)])
+                    if slots <= lane < 2 * slots - 1:
+                        final_copy(i, lane - slots + 1 - n_half).start()
                     else:
-                        ps[q, :, lanes] = acc[buf, :, lanes].astype(jnp.bfloat16)
-                        final_copy(q, u).start()
-
-        def down_dot(src, item, q):
-            def body(i, carry):
-                at = pl.ds(pl.multiple_of(i * row_tile, row_tile), row_tile)
-                acc[item % 2, at, pl.ds(0, cols * pieces)] = dot(src[at, :], vb[q])
-                return carry
-
-            lax.fori_loop(0, row_tiles, body, 0)
-
-        def own_step(q, carry):
-            for piece in range(1, pieces):
-                stages = stages_from(piece, down_bits)
-                if stages:
-                    down_arrival(q, piece).wait_recv()
-                    for stage in stages:
-                        down_copy(q, piece, stage).start()
-                    v_local(q, piece).start()
-            v_local(q, 0).start()
-
-            @pl.when(q > 0)
-            def _():
-                chain(q - 1, q - 1, True)
-
-            for piece in range(1, pieces):
-                if not stages_from(piece, down_bits):
-                    down_arrival(q, piece).wait_recv()
-                    v_local(q, piece).start()
-            for piece in range(pieces):
-                v_local(q, piece).wait()
-            down_dot(hid, q, q)
-            return carry
-
-        lax.fori_loop(0, col_chunks, own_step, 0)
-        chain(col_chunks - 1, col_chunks - 1, True)
-
-        def hidden_arrives(j, carry):
-            hidden_copy(j).wait_recv()
-            return carry
-
-        lax.fori_loop(0, chunks, hidden_arrives, 0)
-
-        def other_step(q, carry):
-            down_dot(hx, col_chunks + q, q)
-
-            @pl.when(q > 0)
-            def _():
-                chain(col_chunks + q - 1, q - 1, False)
-            return carry
-
-        lax.fori_loop(0, col_chunks, other_step, 0)
-        chain(2 * col_chunks - 1, col_chunks - 1, False)
+                        deliver(i, src)
+
+        def down_dot(src, i, other):
+            q = i // ROW_SPLIT
+            ps[q + col_chunks * other, rows_of(i), pl.ds(0, cols * pieces)] = dot(src[rows_of(i), :], vb[q]).astype(jnp.bfloat16)
+
+        def down_step(s, carry):
+            q = s // ROW_SPLIT
+            fresh = (s < items) & (s % ROW_SPLIT == 0)
+
+            @pl.when(fresh)
+            def _():
+                for piece in range(1, pieces):
+                    stages = stages_from(piece, down_bits)
+                    if stages:
+                        down_arrival(q, piece).wait_recv()
+                        for stage in stages:
+                            down_copy(q, piece, stage).start()
+                        v_local(q, piece).start()
+                v_local(q, 0).start()
+
+            for lane in range(2 * slots):
+                chain(s, lane)
+
+            @pl.when(fresh)
+            def _():
+                for piece in range(1, pieces):
+                    if not stages_from(piece, down_bits):
+                        down_arrival(q, piece).wait_recv()
+                        v_local(q, piece).start()
+                for piece in range(pieces):
+                    v_local(q, piece).wait()
+
+            @pl.when(s == items)
+            def _():
+                for j in range(chunks):
+                    hidden_copy(j).wait_recv()
+
+            @pl.when(s < items)
+            def _():
+                down_dot(hid, s, 0)
+
+            @pl.when((s >= items) & (s < 2 * items))
+            def _():
+                down_dot(hx, s - items, 1)
+                cross_copy(s - items).start()
+            return carry
+
+        lax.fori_loop(0, 2 * items + planes + 2, down_step, 0)
 
         @pl.when(z % 2 != n_half)
         def _():
-            def body(q, carry):
-                final_copy(q, 0).wait_recv()
-                deliver(q, lambda at, c: fr[q, at, pl.ds(c * cols, cols)].astype(jnp.float32))
+            def body(i, carry):
+                @pl.when(z != entering)
+                def _():
+                    final_copy(i, 0).wait_recv()
+                    deliver(i, fr.at[i])
                 return carry
 
-            lax.fori_loop(0, col_chunks, body, 0)
+            lax.fori_loop(0, items, body, 0)
 
         write = pltpu.make_async_copy(ob, out, misc_sem.at[0])
         write.start()
@@ -481,17 +525,26 @@
             for piece in range(pieces):
                 for stage in stages_from(piece, down_bits):
                     down_copy(q, piece, stage).wait_send()
-            for u in range(slots):
-                @pl.when(z != target(u))
-                def _():
-                    z_up(col_chunks + q, q, u).wait_send()
-
-                @pl.when(z == target(u))
-                def _():
-                    final_copy(q, u).wait_send()
             return carry
 
         lax.fori_loop(0, col_chunks, settle_down, 0)
+
+        def settle_sums(i, carry):
+            cross_copy(i).wait_send()
+            for lane in range(2 * slots):
+                src, to = lane_source(i, lane)
+
+                @pl.when(z != to)
+                def _():
+                    z_copy(i, lane, src, True).wait_send()
+
+                if slots <= lane < 2 * slots - 1:
+                    @pl.when(z == to)
+                    def _():
+                        final_copy(i, lane - slots + 1 - n_half).wait_send()
+            return carry
+
+        lax.fori_loop(0, items, settle_sums, 0)
 
         def settle_hidden(j, carry):
             hidden_copy(j).wait_send()
@@ -518,6 +571,7 @@
         chunks, col_chunks = hidden // hj, out_block // cols
         half, shard = width // 2, rows // planes
         slab = cols * pieces
+        items, part = col_chunks * ROW_SPLIT, rows // ROW_SPLIT
         bf, f32 = jnp.bfloat16, jnp.float32
         dma = pltpu.SemaphoreType.DMA
         shared = (chunks, half, hj) == (col_chunks, hidden, slab)
@@ -527,14 +581,15 @@
             pltpu.VMEM((rows, half), bf),
             pltpu.VMEM((rows, half), bf),
             pltpu.VMEM((chunks, half, hj), bf),
-            pltpu.VMEM((max(chunks, col_chunks), rows, max(hj, slab)), bf),
+            pltpu.VMEM((max(chunks, 2 * col_chunks), rows, max(hj, slab)), bf),
             pltpu.VMEM((chunks, rows, hj), bf),
-            pltpu.VMEM((2, rows, max(hj, slab)), f32),
+            pltpu.VMEM((rows, hj), f32),
             pltpu.VMEM((rows, hidden), bf),
             pltpu.VMEM((rows, hidden), bf),
-            pltpu.VMEM((2 * col_chunks, slots, rows, per_plane * cols), bf),
-            pltpu.VMEM((2 * col_chunks, slots, rows, per_plane * cols), bf),
-            pltpu.VMEM((col_chunks, rows, per_plane * cols), bf),
+            pltpu.VMEM((2 * slots, items, part, per_plane * cols), bf),
+            pltpu.VMEM((2 * slots, items, part, per_plane * cols), bf),
+            pltpu.VMEM((items, part, per_plane * cols), bf),
+            pltpu.VMEM((items, part, per_plane * cols), bf),
             pltpu.VMEM((rows, own_width), bf),
         ]
         if not shared:
@@ -548,9 +603,9 @@
             dma((col_chunks, pieces - 1)), dma((col_chunks, pieces - 1)),
             dma, dma,
             dma((planes,)), dma((planes,)), dma((planes,)), dma((planes,)),
-            dma((chunks,)), dma((chunks,)), dma((chunks,)), dma((chunks,)),
-            dma((2 * col_chunks, slots)), dma((2 * col_chunks, slots)), dma((2 * col_chunks, slots)),
-            dma((2, col_chunks)),
+            dma((chunks, planes)), dma((chunks, planes)), dma((chunks,)), dma((chunks,)),
+            dma((2 * slots, items)), dma((2 * slots, items)), dma((2 * slots, items)),
+            dma((2, items)), dma((2, items)),
         ]
         hbm = pl.BlockSpec(memory_space=pltpu.HBM)
         result, _ = pl.pallas_call(

time: 515 us -> 299 us (0.58)
  the two profiles are of different devices: /device:TPU:18 before, /device:TPU:6 now
where the time goes in v1:
time: 299 us; the launch traced here: 297 us
  Pallas kernels  292 us (98%)
  local copies, waits for them, and re-layouts  5.28 us (2%)
    pallas_call x1, Pallas kernels, per_device(): pl.pallas_call(kernel, out_shape=(jax.ShapeDtypeStruct((rows, own_width),...  292 us

profile of v1, /device:TPU:6, one launch (start us, length us, event | category | flops | bytes accessed | tf_op | source)
XLA Modules:
  0.0 297.1 jit_solution(9559051796846373805)
XLA Ops:
  0.0 1.3 broadcast_in_dim.11.dbias
  1.3 1.3 broadcast_in_dim.9.gain
  2.6 291.8 %shard_map.64 = (bf16[512,1536]{1,0:T(8,128)(2,1)}, bf16[6,3072,512]{2,1,0:T(8,128)(2,1)}) custom-call(bf16[512,6144]{1,0:T(8,128)(2,1)} %tok.1, bf16[1,6144]{1,0:T(2,128)(2,1)} %broadcast_in_dim.9.gain, bf16[768,3072]{1,0:T(8,128)(2,1)} %w.1, f32[1,3072]{1,0:T(1,128)} %bitcast.1, bf16[3072,768]{1,0:T(8,128)(2,1)} %v.1, f32[1,1536]{1,0:T(1,128)} %broadcast_in_dim.11.dbias), custom_call_target="tpu_custom_call" | custom-call | tf_op jit(solution)/shard_map/pallas_call | solution.py:611
  294.5 2.7 copy.8

commit v2 on v1

--- a/solution.py
+++ b/solution.py
@@ -19,6 +19,26 @@
     while extent % step:
         step -= 128
     return step
+
+
+def order_of(col_chunks, splits):
+    own = [(0, q, h) for q in range(col_chunks) for h in range(splits)]
+    last = col_chunks - 1
+    other = [(1, q, 0) for q in range(last)]
+    later = [(1, q, h) for h in range(1, splits) for q in range(col_chunks)]
+    other += later[:3] + [(1, last, 0)] + later[3:]
+    order, loaded, turn = [], -1, 0
+    while own or other:
+        ready = other and other[0][1] <= loaded and len(order) >= 2 * splits
+        if own and (turn == 0 or not ready):
+            order.append(own.pop(0))
+            loaded, turn = order[-1][1], 1
+        elif ready:
+            order.append(other.pop(0))
+            turn = 0
+        if len(order) < 2 * splits:
+            turn = 0
+    return order
 
 
 def dot(a, b):
@@ -274,10 +294,17 @@
                 send_sem=p_send.at[j, block], recv_sem=p_recv.at[j, block],
                 device_id=near(k_bit), device_id_type=MESH)
 
-        def hidden_copy(j):
+        part = rows // ROW_SPLIT
+        items = col_chunks * ROW_SPLIT
+
+        def rows_of(i):
+            return pl.ds(pl.multiple_of((i % ROW_SPLIT) * part, part), part)
+
+        def hidden_copy(j, h):
             place = pl.ds(pl.multiple_of(j * hj, hj), hj)
             return pltpu.make_async_remote_copy(
-                src_ref=hid.at[:, place], dst_ref=hx.at[:, place], send_sem=h_send.at[j], recv_sem=h_recv.at[j],
+                src_ref=hid.at[rows_of(h), place], dst_ref=hx.at[rows_of(h), place],
+                send_sem=h_send.at[j, h], recv_sem=h_recv.at[j, h],
                 device_id=near(n_bit), device_id_type=MESH)
 
         row_tile = min(256, rows)
@@ -301,7 +328,7 @@
                 return carry
 
             lax.fori_loop(0, rows // 64, body, 0)
-            hidden_copy(j).start()
+            hidden_copy(j, 0).start()
 
         rounds = max(planes, chunks)
 
@@ -374,13 +401,18 @@
         small[2].wait()
         small[3].wait()
 
-        part = rows // ROW_SPLIT
-        items = col_chunks * ROW_SPLIT
         crossed = n_half * (slots - 1)
         entering = 2 * ((1 - n_half) * (slots - 1)) + 1 - n_half
-
-        def rows_of(i):
-            return pl.ds(pl.multiple_of((i % ROW_SPLIT) * part, part), part)
+        order = order_of(col_chunks, ROW_SPLIT)
+        first_other = [k for k in range(len(order)) if order[k][0]][0]
+        late_hidden = [(j, h) for h in range(1, ROW_SPLIT) for j in range(chunks)]
+
+        def code_of(s):
+            code = -1
+            for k in range(len(order)):
+                kind, q, h = order[k]
+                code = jnp.where(s == k, kind * items + q * ROW_SPLIT + h, code)
+            return code
 
         def lanes_of(u):
             return pl.ds(pl.multiple_of(u * slot_width, slot_width), slot_width)
@@ -425,8 +457,9 @@
 
         def chain(s, lane):
             _, to = lane_source(0, lane)
-            late = 1 if lane < slots else items + 1 if lane < 2 * slots - 1 else items + 2
-            i = s - late - depth_of(to)
+            late = 2 if lane == 2 * slots - 1 else 1
+            code = code_of(s - late - depth_of(to))
+            i = code if lane < slots else code - items
 
             @pl.when((i >= 0) & (i < items))
             def _():
@@ -464,8 +497,11 @@
             ps[q + col_chunks * other, rows_of(i), pl.ds(0, cols * pieces)] = dot(src[rows_of(i), :], vb[q]).astype(jnp.bfloat16)
 
         def down_step(s, carry):
-            q = s // ROW_SPLIT
-            fresh = (s < items) & (s % ROW_SPLIT == 0)
+            code = code_of(s)
+            i = code % items
+            q = i // ROW_SPLIT
+            own, other = (code >= 0) & (code < items), code >= items
+            fresh = own & (i % ROW_SPLIT == 0)
 
             @pl.when(fresh)
             def _():
@@ -490,19 +526,24 @@
                 for piece in range(pieces):
                     v_local(q, piece).wait()
 
-            @pl.when(s == items)
+            for k in range(len(late_hidden)):
+                @pl.when(s == first_other + k + (k + 1) // 2)
+                def _():
+                    hidden_copy(*late_hidden[k]).start()
+
+            @pl.when(other & (q == 0))
             def _():
                 for j in range(chunks):
-                    hidden_copy(j).wait_recv()
-
-            @pl.when(s < items)
-            def _():
-                down_dot(hid, s, 0)
-
-            @pl.when((s >= items) & (s < 2 * items))
-            def _():
-                down_dot(hx, s - items, 1)
-                cross_copy(s - items).start()
+                    hidden_copy(j, i % ROW_SPLIT).wait_recv()
+
+            @pl.when(own)
+            def _():
+                down_dot(hid, i, 0)
+
+            @pl.when(other)
+            def _():
+                down_dot(hx, i, 1)
+                cross_copy(i).start()
             return carry
 
         lax.fori_loop(0, 2 * items + planes + 2, down_step, 0)
@@ -547,7 +588,8 @@
         lax.fori_loop(0, items, settle_sums, 0)
 
         def settle_hidden(j, carry):
-            hidden_copy(j).wait_send()
+            for h in range(ROW_SPLIT):
+                hidden_copy(j, h).wait_send()
             return carry
 
         lax.fori_loop(0, chunks, settle_hidden, 0)
@@ -603,7 +645,7 @@
             dma((col_chunks, pieces - 1)), dma((col_chunks, pieces - 1)),
             dma, dma,
             dma((planes,)), dma((planes,)), dma((planes,)), dma((planes,)),
-            dma((chunks, planes)), dma((chunks, planes)), dma((chunks,)), dma((chunks,)),
+            dma((chunks, planes)), dma((chunks, planes)), dma((chunks, ROW_SPLIT)), dma((chunks, ROW_SPLIT)),
             dma((2 * slots, items)), dma((2 * slots, items)), dma((2 * slots, items)),
             dma((2, items)), dma((2, items)),
         ]

time: 299 us -> 276 us (0.923)
  Pallas kernels: 292 us -> 270 us
    pallas_call x1, Pallas kernels: 292 us -> 270 us  [per_device(): pl.pallas_call(kernel, out_shape=(jax.ShapeDtypeStruct((rows, own_width),...]
where the time goes in v2:
time: 276 us; the launch traced here: 275 us
  Pallas kernels  270 us (98%)
  local copies, waits for them, and re-layouts  5.28 us (2%)
    pallas_call x1, Pallas kernels, per_device(): pl.pallas_call(kernel, out_shape=(jax.ShapeDtypeStruct((rows, own_width),...  270 us

profile of v2, /device:TPU:6, one launch (start us, length us, event | category | flops | bytes accessed | tf_op | source)
XLA Modules:
  0.0 275.3 jit_solution(14618889395445356402)
XLA Ops:
  0.0 1.3 broadcast_in_dim.11.dbias
  1.3 1.3 broadcast_in_dim.9.gain
  2.6 270.0 %shard_map.64 = (bf16[512,1536]{1,0:T(8,128)(2,1)}, bf16[6,3072,512]{2,1,0:T(8,128)(2,1)}) custom-call(bf16[512,6144]{1,0:T(8,128)(2,1)} %tok.1, bf16[1,6144]{1,0:T(2,128)(2,1)} %broadcast_in_dim.9.gain, bf16[768,3072]{1,0:T(8,128)(2,1)} %w.1, f32[1,3072]{1,0:T(1,128)} %bitcast.1, bf16[3072,768]{1,0:T(8,128)(2,1)} %v.1, f32[1,1536]{1,0:T(1,128)} %broadcast_in_dim.11.dbias), custom_call_target="tpu_custom_call" | custom-call | tf_op jit(solution)/shard_map/pallas_call | solution.py:653
  272.6 2.7 copy.8

commit v3 on v2

--- a/solution.py
+++ b/solution.py
@@ -11,6 +11,9 @@
 HID_CHUNK = 512
 COL_CHUNK = 128
 ROW_SPLIT = 2
+HOP_STEPS = 2
+CROSS_STEPS = 2
+FIRST_HIDDEN = 1
 EARLY_V = (-1, 1)
 
 
@@ -21,23 +24,32 @@
     return step
 
 
-def order_of(col_chunks, splits):
-    own = [(0, q, h) for q in range(col_chunks) for h in range(splits)]
-    last = col_chunks - 1
-    other = [(1, q, 0) for q in range(last)]
-    later = [(1, q, h) for h in range(1, splits) for q in range(col_chunks)]
-    other += later[:3] + [(1, last, 0)] + later[3:]
-    order, loaded, turn = [], -1, 0
+def order_of(col_chunks, splits, chunks):
+    def columns_at(q):
+        return 0 if q < 2 else int(splits * (3.25 + 2 * (q - 2)))
+
+    def hidden_at(h):
+        return 2 + 2 * chunks * h if h else FIRST_HIDDEN * splits
+
+    own = [(0, q, h) for h in range(splits) for q in range(min(2, col_chunks))]
+    own += [(0, q, h) for q in range(2, col_chunks) for h in range(splits)]
+    other = [(1, q, h) for q in range(col_chunks) for h in range(splits)]
+    other.sort(key=lambda item: (max(columns_at(item[1]), hidden_at(item[2])), item[2], item[1]))
+    order, loaded, load = [], set(), [0, 0]
     while own or other:
-        ready = other and other[0][1] <= loaded and len(order) >= 2 * splits
-        if own and (turn == 0 or not ready):
-            order.append(own.pop(0))
-            loaded, turn = order[-1][1], 1
-        elif ready:
-            order.append(other.pop(0))
-            turn = 0
-        if len(order) < 2 * splits:
-            turn = 0
+        here = len(order)
+        known = [item for item in other if item[1] in loaded]
+        ready = [item for item in known if max(columns_at(item[1]), hidden_at(item[2])) <= here]
+        own_ready = own and columns_at(own[0][1]) <= here
+        if own and (own_ready and (not ready or load[0] <= load[1]) or not (own_ready or ready)):
+            pick = own.pop(0)
+            loaded.add(pick[1])
+        else:
+            pick = (ready or known)[0]
+            other.remove(pick)
+        load[pick[0]] += 2
+        load[1 - pick[0]] += 1
+        order.append(pick)
     return order
 
 
@@ -70,8 +82,8 @@
         tk, sh, xo, xp, wb, ps, pr, acc, hid, hx, zu, zd, fr, cr, ob, *rest,
     ):
         rest = list(rest)
-        vb = rest.pop(0) if len(rest) == 27 else wb
-        (gv, ub, db, tk_sem, misc_sem, wl_sem, vl_sem,
+        vb = rest.pop(0) if len(rest) == 29 else wb
+        (gv, ub, db, gain_row, bias_row, tk_sem, misc_sem, wl_sem, vl_sem,
          up_send, up_recv, dn_send, dn_recv, x_send, x_recv,
          zxu_send, zxu_recv, zxd_send, zxd_recv,
          p_send, p_recv, h_send, h_recv, z_send, zu_recv, zd_recv, f_sem, c_sem) = rest
@@ -179,9 +191,9 @@
         token_copy(-1, 0).start()
         token_copy(0, 1).start()
         small = [
-            pltpu.make_async_copy(gain, gv, misc_sem.at[0]),
+            pltpu.make_async_copy(gain, gain_row, misc_sem.at[0]),
             pltpu.make_async_copy(ubias, ub, misc_sem.at[1]),
-            pltpu.make_async_copy(dbias, db, misc_sem.at[2]),
+            pltpu.make_async_copy(dbias, bias_row, misc_sem.at[2]),
             pltpu.make_async_copy(
                 tok.at[:, pl.ds(pl.multiple_of(z * own_width, own_width), own_width)], ob, misc_sem.at[3]),
         ]
@@ -199,6 +211,7 @@
 
         lax.fori_loop(0, chunks, start_up, 0)
         small[0].wait()
+        gv[...] = gain_row[...].reshape(1, width)
 
         tile = 16
 
@@ -287,10 +300,12 @@
 
         small[1].wait()
 
+        parked = ps.shape[0] - chunks
+
         def partial_copy(j, block):
             place = pl.ds(pl.multiple_of(block * shard, shard), shard)
             return pltpu.make_async_remote_copy(
-                src_ref=ps.at[j, place, pl.ds(0, hj)], dst_ref=pr.at[j, place, :],
+                src_ref=ps.at[parked + j, place, pl.ds(0, hj)], dst_ref=pr.at[j, place, :],
                 send_sem=p_send.at[j, block], recv_sem=p_recv.at[j, block],
                 device_id=near(k_bit), device_id_type=MESH)
 
@@ -309,30 +324,33 @@
 
         row_tile = min(256, rows)
 
-        def finish(j):
+        def finish(j, h):
             place = pl.ds(pl.multiple_of(j * hj, hj), hj)
-
-            def kept(i, carry):
-                at = pl.ds(pl.multiple_of(i * row_tile, row_tile), row_tile)
-                acc[at, :] = dot(xo[at, :], wb[j])
+            acc[...] = dot(xo[rows_of(h), :], wb[j])
+            for block in range(planes // ROW_SPLIT):
+                partial_copy(j, h * (planes // ROW_SPLIT) + block).wait_recv()
+            pre = acc[...] + pr[j, rows_of(h), :].astype(jnp.float32) + ub[:, place]
+            hid[rows_of(h), place] = jax.nn.gelu(pre, approximate=True).astype(jnp.bfloat16)
+
+            @pl.when(h == 0)
+            def _():
+                hidden_copy(j, 0).start()
+
+        def finish_rows(j, first, last):
+            def body(h, carry):
+                finish(j, h)
                 return carry
 
-            lax.fori_loop(0, rows // row_tile, kept, 0)
-            for block in range(planes):
-                partial_copy(j, block).wait_recv()
-
-            def body(i, carry):
-                at = pl.ds(pl.multiple_of(i * 64, 64), 64)
-                pre = acc[at, :] + pr[j, at, :].astype(jnp.float32) + ub[:, place]
-                hid[at, place] = jax.nn.gelu(pre, approximate=True).astype(jnp.bfloat16)
-                return carry
-
-            lax.fori_loop(0, rows // 64, body, 0)
-            hidden_copy(j, 0).start()
+            lax.fori_loop(first, last, body, 0)
 
         rounds = max(planes, chunks)
 
         def up_step(m, carry):
+            for j in range(2):
+                @pl.when((m >= planes) & (2 * (m - planes) + j < chunks - 1))
+                def _():
+                    finish_rows(2 * (m - planes) + j, 0, ROW_SPLIT)
+
             @pl.when(m < chunks)
             def _():
                 for piece in range(1, pieces):
@@ -357,11 +375,14 @@
                 distance = jnp.where(t // 2 < m, t // 2, m)
                 j = jnp.where(t // 2 <= m, m, t // 2 - m - 1)
                 block = jnp.where(t % 2 == 0, z - distance, z + distance)
-
-                @pl.when((block >= 0) & (block < planes) & (j < chunks) & ((t % 2 == 0) | (distance > 0)))
+                straight = m >= planes
+                block = jnp.where(straight, t, block)
+                j = jnp.where(straight, m, j)
+
+                @pl.when((block >= 0) & (block < planes) & (j < chunks) & (straight | (t % 2 == 0) | (distance > 0)))
                 def _():
                     at = pl.ds(pl.multiple_of(block * shard, shard), shard)
-                    ps[j, at, pl.ds(0, hj)] = dot(xp[at, :], wb[j]).astype(jnp.bfloat16)
+                    ps[parked + j, at, pl.ds(0, hj)] = dot(xp[at, :], wb[j]).astype(jnp.bfloat16)
                     partial_copy(j, block).start()
                 return carry
 
@@ -371,10 +392,6 @@
                 def _():
                     start_down(q)
 
-            for j in range(2):
-                @pl.when((m >= planes) & (2 * (m - planes) + j < chunks))
-                def _():
-                    finish(2 * (m - planes) + j)
             return carry
 
         lax.fori_loop(0, rounds, up_step, 0)
@@ -383,27 +400,26 @@
         lax.fori_loop(0, col_chunks, start_down_core, 0)
 
         def finish_rest(j, carry):
-            finish(j)
-            return carry
-
-        lax.fori_loop(min(2 * (rounds - planes), chunks), chunks, finish_rest, 0)
+            finish_rows(j, 0, jnp.where(j == chunks - 1, 1, ROW_SPLIT))
+            return carry
+
+        lax.fori_loop(min(2 * (rounds - planes), chunks - 1), chunks, finish_rest, 0)
         shard_send.wait_send()
 
         def settle_up(j, carry):
             for piece in range(pieces):
                 for stage in stages_from(piece, up_bits):
                     up_copy(j, piece, stage).wait_send()
-            for block in range(planes):
-                partial_copy(j, block).wait_send()
             return carry
 
         lax.fori_loop(0, chunks, settle_up, 0)
         small[2].wait()
+        db[...] = bias_row[...].reshape(1, own_width)
         small[3].wait()
 
         crossed = n_half * (slots - 1)
         entering = 2 * ((1 - n_half) * (slots - 1)) + 1 - n_half
-        order = order_of(col_chunks, ROW_SPLIT)
+        order = order_of(col_chunks, ROW_SPLIT, chunks)
         first_other = [k for k in range(len(order)) if order[k][0]][0]
         late_hidden = [(j, h) for h in range(1, ROW_SPLIT) for j in range(chunks)]
 
@@ -457,8 +473,8 @@
 
         def chain(s, lane):
             _, to = lane_source(0, lane)
-            late = 2 if lane == 2 * slots - 1 else 1
-            code = code_of(s - late - depth_of(to))
+            late = CROSS_STEPS if lane == 2 * slots - 1 else 1
+            code = code_of(s - late - HOP_STEPS * depth_of(to))
             i = code if lane < slots else code - items
 
             @pl.when((i >= 0) & (i < items))
@@ -526,10 +542,21 @@
                 for piece in range(pieces):
                     v_local(q, piece).wait()
 
-            for k in range(len(late_hidden)):
-                @pl.when(s == first_other + k + (k + 1) // 2)
-                def _():
-                    hidden_copy(*late_hidden[k]).start()
+            for h in range(1, ROW_SPLIT):
+                @pl.when(s == 2 * h)
+                def _():
+                    finish(chunks - 1, h)
+
+            @pl.when((s >= 2) & (s % 2 == 0) & (s < 2 + 2 * len(late_hidden)))
+            def _():
+                k = s // 2 - 1
+                hidden_copy(k % chunks, k // chunks + 1).start()
+
+            @pl.when(s == first_other)
+            def _():
+                for j in range(chunks):
+                    for block in range(planes):
+                        partial_copy(j, block).wait_send()
 
             @pl.when(other & (q == 0))
             def _():
@@ -546,7 +573,7 @@
                 cross_copy(i).start()
             return carry
 
-        lax.fori_loop(0, 2 * items + planes + 2, down_step, 0)
+        lax.fori_loop(0, 2 * items + HOP_STEPS * (planes - 1) + CROSS_STEPS, down_step, 0)
 
         @pl.when(z % 2 != n_half)
         def _():
@@ -625,7 +652,7 @@
             pltpu.VMEM((chunks, half, hj), bf),
             pltpu.VMEM((max(chunks, 2 * col_chunks), rows, max(hj, slab)), bf),
             pltpu.VMEM((chunks, rows, hj), bf),
-            pltpu.VMEM((rows, hj), f32),
+            pltpu.VMEM((part, hj), f32),
             pltpu.VMEM((rows, hidden), bf),
             pltpu.VMEM((rows, hidden), bf),
             pltpu.VMEM((2 * slots, items, part, per_plane * cols), bf),
@@ -640,6 +667,8 @@
             pltpu.VMEM((1, width), bf),
             pltpu.VMEM((1, hidden), f32),
             pltpu.VMEM((1, own_width), f32),
+            pltpu.VMEM((width,), bf),
+            pltpu.VMEM((own_width,), f32),
             dma((2,)), dma((4,)), dma((chunks,)), dma((col_chunks, pieces)),
             dma((chunks, pieces - 1)), dma((chunks, pieces - 1)),
             dma((col_chunks, pieces - 1)), dma((col_chunks, pieces - 1)),
@@ -661,7 +690,7 @@
             scratch_shapes=scratch,
             compiler_params=pltpu.CompilerParams(
                 collective_id=0, has_side_effects=True, vmem_limit_bytes=67043328),
-        )(tokens, norm_gain[None, :], up_weight, up_bias[None, :], down_weight, down_bias[None, :])
+        )(tokens, norm_gain, up_weight, up_bias[None, :], down_weight, down_bias)
         return result
 
     return per_device

time: 276 us -> 261 us (0.946)
  Pallas kernels: 270 us -> 258 us
    pallas_call x1, Pallas kernels: 270 us -> 258 us  [per_device(): pl.pallas_call(kernel, out_shape=(jax.ShapeDtypeStruct((rows, own_width),...]
where the time goes in v3:
time: 261 us
  Pallas kernels  258 us (99%)
  local copies, waits for them, and re-layouts  2.65 us (1%)
    pallas_call x1, Pallas kernels, per_device(): pl.pallas_call(kernel, out_shape=(jax.ShapeDtypeStruct((rows, own_width),...  258 us

profile of v3, /device:TPU:6, one launch (start us, length us, event | category | flops | bytes accessed | tf_op | source)
XLA Modules:
  0.0 260.5 jit_solution(14167288930815011897)
XLA Ops:
  0.0 257.9 %shard_map.64 = (bf16[512,1536]{1,0:T(8,128)(2,1)}, bf16[6,3072,512]{2,1,0:T(8,128)(2,1)}) custom-call(bf16[512,6144]{1,0:T(8,128)(2,1)} %tok.1, bf16[6144]{0:T(1024)(128)(2,1)} %gain.1, bf16[768,3072]{1,0:T(8,128)(2,1)} %w.1, f32[1,3072]{1,0:T(1,128)} %bitcast.1, bf16[3072,768]{1,0:T(8,128)(2,1)} %v.1, f32[1536]{0:T(1024)} %dbias.1), custom_call_target="tpu_custom_call" | custom-call | tf_op jit(solution)/shard_map/pallas_call | solution.py:682
  257.9 2.7 %copy.8 = bf16[512,1536]{1,0:T(8,128)(2,1)} copy(bf16[512,1536]{1,0:T(8,128)(2,1)} %get-tuple-element.6) | data formatting | bytes 3145728

commit v4 on v3

--- a/solution.py
+++ b/solution.py
@@ -12,6 +12,7 @@
 COL_CHUNK = 128
 ROW_SPLIT = 2
 HOP_STEPS = 2
+DELIVER_STEPS = 8
 CROSS_STEPS = 2
 FIRST_HIDDEN = 1
 EARLY_V = (-1, 1)
@@ -508,6 +509,14 @@
                     else:
                         deliver(i, src)
 
+        def take_final(s):
+            i = code_of(s - DELIVER_STEPS) - items
+
+            @pl.when((i >= 0) & (z % 2 != n_half) & (z != entering))
+            def _():
+                final_copy(i, 0).wait_recv()
+                deliver(i, fr.at[i])
+
         def down_dot(src, i, other):
             q = i // ROW_SPLIT
             ps[q + col_chunks * other, rows_of(i), pl.ds(0, cols * pieces)] = dot(src[rows_of(i), :], vb[q]).astype(jnp.bfloat16)
@@ -532,6 +541,7 @@
 
             for lane in range(2 * slots):
                 chain(s, lane)
+            take_final(s)
 
             @pl.when(fresh)
             def _():
@@ -573,18 +583,7 @@
                 cross_copy(i).start()
             return carry
 
-        lax.fori_loop(0, 2 * items + HOP_STEPS * (planes - 1) + CROSS_STEPS, down_step, 0)
-
-        @pl.when(z % 2 != n_half)
-        def _():
-            def body(i, carry):
-                @pl.when(z != entering)
-                def _():
-                    final_copy(i, 0).wait_recv()
-                    deliver(i, fr.at[i])
-                return carry
-
-            lax.fori_loop(0, items, body, 0)
+        lax.fori_loop(0, 2 * items + max(HOP_STEPS * (planes - 1) + CROSS_STEPS, DELIVER_STEPS), down_step, 0)
 
         write = pltpu.make_async_copy(ob, out, misc_sem.at[0])
         write.start()

time: 261 us -> 261 us (level)
  no operation moved by 1% of the time
where the time goes in v4:
time: 261 us; the launch traced here: 260 us
  Pallas kernels  258 us (99%)
  local copies, waits for them, and re-layouts  2.65 us (1%)
    pallas_call x1, Pallas kernels, per_device(): pl.pallas_call(kernel, out_shape=(jax.ShapeDtypeStruct((rows, own_width),...  258 us

profile of v4, /device:TPU:6, one launch (start us, length us, event | category | flops | bytes accessed | tf_op | source)
XLA Modules:
  0.0 260.4 jit_solution(12422587630779536938)
XLA Ops:
  0.0 257.7 %shard_map.64 = (bf16[512,1536]{1,0:T(8,128)(2,1)}, bf16[6,3072,512]{2,1,0:T(8,128)(2,1)}) custom-call(bf16[512,6144]{1,0:T(8,128)(2,1)} %tok.1, bf16[6144]{0:T(1024)(128)(2,1)} %gain.1, bf16[768,3072]{1,0:T(8,128)(2,1)} %w.1, f32[1,3072]{1,0:T(1,128)} %bitcast.1, bf16[3072,768]{1,0:T(8,128)(2,1)} %v.1, f32[1536]{0:T(1024)} %dbias.1), custom_call_target="tpu_custom_call" | custom-call | tf_op jit(solution)/shard_map/pallas_call | solution.py:681
  257.7 2.7 %copy.8 = bf16[512,1536]{1,0:T(8,128)(2,1)} copy(bf16[512,1536]{1,0:T(8,128)(2,1)} %get-tuple-element.6) | data formatting | bytes 3145728
